TPU v7x, 32 devices: a whole 2x2x4 slice. The times are simulated.
32 devices in a mesh: group: 2 (over y), station: 4 (over z), tm: 2 (over x), chan: 2 (over core).
Axes of the slice: x: 2, y: 2, z: 4, core: 2. Of those that a mesh axis runs over, the one named last changes fastest.
Arguments:
- voltages: bfloat16 [8, 128, 2, 96, 256], P(('group', 'station'), 'chan', None, None, 'tm'), parts along dimension 0, may hold values from -6 to 6
- delays: int32 [8], P(('group', 'station')), parts along dimension 0, may hold values from 0 to 16, as said below
- tap_sets: int32 [8, 128], P(('group', 'station'), 'chan'), parts along dimension 0, may hold values from 0 to 15
- tap_table: bfloat16 [16, 16], replicated, may hold values from -1.5 to 1.5
- weights: bfloat16 [8, 128, 2, 96, 128], P(('group', 'station'), 'chan'), parts along dimension 0, may hold values from -0.3125 to 0.3125
Outputs:
- array_beams: bfloat16 [256, 2, 128, 256], P(('group', 'chan', 'station'), None, None, 'tm'), parts along dimension 0
There are 2 independent parts, one for each index of `group`. A program takes and returns all parts, laid end to end along the dimension named above; an argument that names none is the same for every part. Nothing has to cross between parts.
Inputs may be any that keep to these rules, and one draw needn't show every extreme that they name: `delays`: every delay lies in 0 to 16, and some station has delay 16.
All inputs are finite; a program needn't handle non-finite values.
Results may differ from a plain program's by a relative error of at most 0.0049.
Values may be sent and summed in bfloat16 or wider, within the bound.
A program may use at most 64 MiB of HBM per device.

v0:
```python
import functools

import jax
import jax.numpy as jnp
from jax import lax
from jax.experimental import pallas as pl
from jax.experimental.pallas import tpu as pltpu
from jax.sharding import PartitionSpec as P

MAXD = 16
MESH = pl.DeviceIdType.MESH
CHUNK = 2


def kernel(
    n, tm_count, sizes, tap_sets, delays, taps, v_hbm, w_hbm, out_buf,
    v_buf, w_buf, band, halo_out, halo_in, acc_out, acc_in,
    v_sem, w_sem, hs_sem, hr_sem, as_sem, ar_sem,
):
    channels, parts, antennas, beams, time_len, chunk, pad = sizes
    rows = channels // n
    half = rows // 2
    per_half = half // chunk
    rows_in = parts * antennas
    folds = time_len // pad
    fold_rows = rows_in // folds
    set_count, tap_count = taps.shape
    items = n * per_half

    me = lax.axis_index("station")
    tm = lax.axis_index("tm")
    right, left = lax.rem(me + 1, n), lax.rem(me + n - 1, n)
    later, earlier = lax.rem(tm + 1, tm_count), lax.rem(tm + tm_count - 1, tm_count)

    def place(it, side):
        step, k = it // per_half, lax.rem(it, per_half)
        odd = lax.rem(step, 2)
        offset = n // 2 - odd - step // 2
        if side == 0:
            block, second = lax.rem(me + offset, n), odd
        else:
            block, second = lax.rem(me + n - offset, n), 1 - odd
        within = second * half + k * chunk
        return block * rows + within, within

    def v_copy(it, side):
        first, _ = place(it, side)
        span = pl.ds(first, chunk)
        return pltpu.make_async_copy(v_hbm.at[span], v_buf.at[span], v_sem.at[it, side])

    def w_copy(it, side):
        first, _ = place(it, side)
        span = pl.ds(first, chunk)
        return pltpu.make_async_copy(w_hbm.at[span], w_buf.at[span], w_sem.at[it, side])

    def halo_copy(it, side):
        return pltpu.make_async_remote_copy(
            src_ref=halo_out.at[it, side],
            dst_ref=halo_in.at[it, side],
            send_sem=hs_sem.at[it, side],
            recv_sem=hr_sem.at[it, side],
            device_id={"tm": later},
            device_id_type=MESH,
        )

    def sum_copy(it, side):
        return pltpu.make_async_remote_copy(
            src_ref=acc_out.at[it, side],
            dst_ref=acc_in.at[it, side],
            send_sem=as_sem.at[it, side],
            recv_sem=ar_sem.at[it, side],
            device_id={"station": right if side == 0 else left},
            device_id_type=MESH,
        )

    def start_loads(it, carry):
        for side in (0, 1):
            v_copy(it, side).start()
            w_copy(it, side).start()
        return carry

    lax.fori_loop(0, items, start_loads, 0)

    barrier = pltpu.get_barrier_semaphore()
    for target in ({"station": left}, {"station": right}, {"tm": earlier}, {"tm": later}):
        pl.semaphore_signal(barrier, inc=1, device_id=target, device_id_type=MESH)

    from_row = lax.broadcasted_iota(jnp.int32, (folds * time_len, time_len), 0)
    to_lane = lax.broadcasted_iota(jnp.int32, (folds * time_len, time_len), 1)
    wanted = (to_lane // pad) * time_len + lax.rem(to_lane, pad) + time_len - pad
    picker = (from_row == wanted).astype(jnp.float32).astype(jnp.bfloat16)

    def pack(it, side):
        first, _ = place(it, side)
        v_copy(it, side).wait()
        for c in range(chunk):
            wide = jnp.concatenate(
                [v_buf[first + c, pl.ds(q * fold_rows, fold_rows), :] for q in range(folds)], axis=1
            )
            halo_out[it, side, c] = jnp.dot(
                wide, picker, preferred_element_type=jnp.float32
            ).astype(jnp.bfloat16)
        halo_copy(it, side).start()

    pl.semaphore_wait(barrier, 4)

    def pack_first(it, carry):
        pack(it, 0)
        pack(it, 1)
        return carry

    lead = per_half
    lax.fori_loop(0, lead, pack_first, 0)

    out_pos = lax.broadcasted_iota(jnp.int32, (time_len, 2 * time_len), 0)
    column = lax.broadcasted_iota(jnp.int32, (time_len, 2 * time_len), 1)
    in_pos = jnp.where(column < time_len, column, lax.rem(column, pad) - pad)
    usable = (column < time_len) | (tm > 0)
    lag = jnp.where(usable, out_pos - delays[0] - in_pos, -1)

    def make_band(m, carry):
        values = jnp.zeros((time_len, 2 * time_len), jnp.float32)
        for k in range(tap_count):
            values = jnp.where(lag == k, taps[m, k], values)
        band[m] = values.astype(jnp.bfloat16)
        return carry

    lax.fori_loop(0, set_count, make_band, 0)

    fold_lane = lax.broadcasted_iota(jnp.int32, (fold_rows, time_len), 1) // pad

    def beams_of(it, side, c):
        first, _ = place(it, side)
        channel = first + c
        rim = halo_in[it, side, c]
        rims = jnp.concatenate(
            [jnp.where(fold_lane == q, rim, jnp.zeros_like(rim)) for q in range(folds)], axis=0
        )
        window = jnp.concatenate([v_buf[channel], rims], axis=1)
        filt = band[tap_sets[0, channel]]
        delayed = lax.dot_general(
            filt, window, (((1,), (1,)), ((), ())), preferred_element_type=jnp.float32
        ).astype(jnp.bfloat16)
        wr = w_buf[channel, pl.ds(0, antennas), :]
        wi = w_buf[channel, pl.ds(antennas, antennas), :]
        steer = jnp.concatenate(
            [jnp.concatenate([wr, wi], axis=1), jnp.concatenate([-wi, wr], axis=1)], axis=0
        )
        return jnp.dot(delayed, steer, preferred_element_type=jnp.float32)

    def ready(it, side):
        halo_copy(it, side).wait_recv()
        w_copy(it, side).wait()

    def head(it, carry):
        for side in (0, 1):
            pack(it + lead, side)
        for side in (0, 1):
            ready(it, side)
            for c in range(chunk):
                acc_out[it, side, c] = beams_of(it, side, c).astype(jnp.bfloat16)
            sum_copy(it, side).start()
        return carry

    lax.fori_loop(0, 2 * per_half, head, 0)

    def middle(it, carry):
        for side in (0, 1):
            pack(it + lead, side)
        for side in (0, 1):
            ready(it, side)
            before = it - 2 * per_half
            sum_copy(before, side).wait_recv()
            for c in range(chunk):
                total = beams_of(it, side, c) + acc_in[before, side, c].astype(jnp.float32)
                acc_out[it, side, c] = total.astype(jnp.bfloat16)
            sum_copy(it, side).start()
        return carry

    lax.fori_loop(2 * per_half, items - per_half, middle, 0)

    def last(it, carry):
        for side in (0, 1):
            ready(it, side)
            _, within = place(it, side)
            same, other = it - 2 * per_half, it - per_half
            sums = [beams_of(it, side, c) for c in range(chunk)]
            sum_copy(same, side).wait_recv()
            sum_copy(other, 1 - side).wait_recv()
            for c in range(chunk):
                total = sums[c] + acc_in[same, side, c].astype(jnp.float32)
                total = total + acc_in[other, 1 - side, c].astype(jnp.float32)
                out_buf[within + c] = total.T.astype(jnp.bfloat16)
        return carry

    lax.fori_loop(items - per_half, items, last, 0)

    def drain_halo(it, carry):
        for side in (0, 1):
            halo_copy(it, side).wait_send()
        return carry

    lax.fori_loop(0, items, drain_halo, 0)

    def drain_sums(it, carry):
        for side in (0, 1):
            sum_copy(it, side).wait_send()
        return carry

    lax.fori_loop(0, items - per_half, drain_sums, 0)


def body(voltages, delays, tap_sets, tap_table, weights):
    _, channels, parts, antennas, time_len = voltages.shape
    beams = weights.shape[-1]
    set_count, tap_count = tap_table.shape
    n = lax.axis_size("station")
    tm_count = lax.axis_size("tm")
    rows = channels // n
    chunk = min(CHUNK, rows // 2)
    per_half = rows // 2 // chunk
    items = n * per_half
    pad = MAXD + tap_count
    rows_in = parts * antennas
    fold_rows = rows_in * pad // time_len
    sizes = (channels, parts, antennas, beams, time_len, chunk, pad)
    sent = items - per_half
    bf16 = jnp.bfloat16
    dma = pltpu.SemaphoreType.DMA
    smem = pl.BlockSpec(memory_space=pltpu.SMEM)
    in_hbm = pl.BlockSpec(memory_space=pltpu.HBM)
    result = pl.pallas_call(
        functools.partial(kernel, n, tm_count, sizes),
        out_shape=jax.ShapeDtypeStruct((rows, 2 * beams, time_len), bf16),
        in_specs=[smem, smem, smem, in_hbm, in_hbm],
        out_specs=pl.BlockSpec(memory_space=pltpu.VMEM),
        scratch_shapes=[
            pltpu.VMEM((channels, rows_in, time_len), bf16),
            pltpu.VMEM((channels, rows_in, beams), bf16),
            pltpu.VMEM((set_count, time_len, 2 * time_len), bf16),
            pltpu.VMEM((items, 2, chunk, fold_rows, time_len), bf16),
            pltpu.VMEM((items, 2, chunk, fold_rows, time_len), bf16),
            pltpu.VMEM((sent, 2, chunk, time_len, 2 * beams), bf16),
            pltpu.VMEM((sent, 2, chunk, time_len, 2 * beams), bf16),
            dma((items, 2)),
            dma((items, 2)),
            dma((items, 2)),
            dma((items, 2)),
            dma((sent, 2)),
            dma((sent, 2)),
        ],
        compiler_params=pltpu.CompilerParams(
            collective_id=0, has_side_effects=True, vmem_limit_bytes=48 * 1024 * 1024
        ),
    )(
        tap_sets,
        delays,
        tap_table.astype(jnp.float32),
        voltages.reshape(channels, rows_in, time_len),
        weights.reshape(channels, rows_in, beams),
    )
    return result.reshape(rows, 2, beams, time_len)


def solution(mesh):
    return jax.shard_map(
        body,
        mesh=mesh,
        in_specs=(
            P(("group", "station"), "chan", None, None, "tm"),
            P(("group", "station")),
            P(("group", "station"), "chan"),
            P(),
            P(("group", "station"), "chan", None, None, None),
        ),
        out_specs=P(("group", "chan", "station"), None, None, "tm"),
        check_vma=False,
    )
```

profile of v0, /device:TPU:0, one launch (start us, length us, event | category | flops | bytes accessed | tf_op | source)
XLA Modules:
  0.0 90.2 jit_solution(17655543318121796924)
XLA Ops:
  0.7 0.7 convert_element_type.3.taps
  1.3 0.0 copy-start
  1.3 1.9 %copy-done = bf16[1,64,2,96,128]{4,3,2,1,0:T(8,128)(2,1)S(1)} copy-done((bf16[1,64,2,96,128]{4,3,2,1,0:T(8,128)(2,1)S(1)}, bf16[1,64,2,96,128]{4,3,2,1,0:T(8,128)(2,1)}, u32[]{:S(2)}) %copy-start) | copy-done | bytes 3145752
  3.2 0.0 copy-start.1
  3.2 0.7 copy-done.1
  3.9 85.3 %shard_map.55 = bf16[16,256,128]{2,1,0:T(8,128)(2,1)S(1)} custom-call(s32[1,64]{1,0:T(1,128)S(1)} %copy-done.1, s32[1]{0:T(128)S(6)} %copy.7.delays, f32[16,16]{1,0:T(8,128)S(1)} %convert_element_type.3.taps, bf16[64,192,128]{2,1,0:T(8,128)(2,1)S(1)} %bitcast.4, bf16[64,192,128]{2,1,0:T(8,128)(2,1)} %bitcast.5), custom_call_target="tpu_custom_call" | custom-call | tf_op jit(solution)/shard_map/pallas_call | solution.py:232
  89.2 1.0 %copy.8 = bf16[16,2,128,128]{3,2,1,0:T(8,128)(2,1)} copy(bf16[16,2,128,128]{3,2,1,0:T(8,128)(2,1)S(1)} %bitcast.3) | data formatting | bytes 2097152
Async XLA Ops:
  1.3 1.9 %copy-start = (bf16[1,64,2,96,128]{4,3,2,1,0:T(8,128)(2,1)S(1)}, bf16[1,64,2,96,128]{4,3,2,1,0:T(8,128)(2,1)}, u32[]{:S(2)}) copy-start(bf16[1,64,2,96,128]{4,3,2,1,0:T(8,128)(2,1)} %param.5) | copy-start | bytes 9437188
  3.2 0.7 copy-start.1
where the time goes:
time: 90.3 us; the launch traced here: 90.2 us
  Pallas kernels  85.3 us (94%)
  local copies, waits for them, and re-layouts  3.52 us (4%)
    pallas_call x1, Pallas kernels, body(): pl.pallas_call(functools.partial(kernel, n, tm_count, sizes), out_shape=j...  85.3 us
    unnamed x5, local copies, waits for them, and re-layouts  3.52 us

commit v1 on v0

v1 whole, which is shorter than its diff:
```python
import functools

import jax
import jax.numpy as jnp
from jax import lax
from jax.experimental import pallas as pl
from jax.experimental.pallas import tpu as pltpu
from jax.sharding import PartitionSpec as P

MAXD = 16
MESH = pl.DeviceIdType.MESH
LEAD = 4
LAG = 4


def kernel(
    n, tm_count, sizes, sets_hbm, delays_hbm, taps_hbm, v_hbm, w_hbm, out_buf,
    sets, delays, taps, spread, lags, v_buf, w_buf, band, halo_out, halo_in,
    acc_out, acc_in, own,
    small_sem, v_sem, w_sem, hs_sem, hr_sem, as_sem, ar_sem,
):
    channels, parts, antennas, beams, time_len, pad = sizes
    rows = channels // n
    rows_in = parts * antennas
    folds = time_len // pad
    fold_rows = rows_in // folds
    set_count, tap_count = taps.shape
    bf16, f32 = jnp.bfloat16, jnp.float32

    me = lax.axis_index("station")
    tm = lax.axis_index("tm")
    later, earlier = lax.rem(tm + 1, tm_count), lax.rem(tm + tm_count - 1, tm_count)

    flip = jnp.where(me >= n // 2, 1, 0)
    place = me + flip * (n - 1 - 2 * me)
    ahead_dir, back_dir = flip, 1 - flip
    ahead_count = (n - 1 - place) * rows
    back_count = (place + 1) * rows
    offset = LAG + ahead_count - back_count

    def channel_of(station, k):
        return (station + flip * (n - 1 - 2 * station)) * rows + k

    def ahead_channel(i):
        return channel_of(n - 1 - i // rows, lax.rem(i, rows))

    def back_channel(j):
        return channel_of(j // rows, lax.rem(j, rows))

    def v_copy(ch):
        return pltpu.make_async_copy(v_hbm.at[ch], v_buf.at[ch], v_sem.at[ch])

    def w_copy(ch):
        return pltpu.make_async_copy(w_hbm.at[ch], w_buf.at[ch], w_sem.at[ch])

    def halo_copy(ch):
        return pltpu.make_async_remote_copy(
            src_ref=halo_out.at[ch],
            dst_ref=halo_in.at[ch],
            send_sem=hs_sem.at[ch],
            recv_sem=hr_sem.at[ch],
            device_id={"tm": later},
            device_id_type=MESH,
        )

    def sum_copy(ch, direction):
        target = me + 1 - 2 * direction
        final = (ch // rows == target) & (direction == 1)
        slot = jnp.where(final, channels + lax.rem(ch, rows), ch)
        return pltpu.make_async_remote_copy(
            src_ref=acc_out.at[ch],
            dst_ref=acc_in.at[slot],
            send_sem=as_sem.at[ch],
            recv_sem=ar_sem.at[slot],
            device_id={"station": target},
            device_id_type=MESH,
        )

    def arrival(ch, direction):
        final = (ch // rows == me) & (direction == 1)
        return jnp.where(final, channels + lax.rem(ch, rows), ch)

    def wait_arrival(slot):
        pltpu.make_async_copy(acc_in.at[slot], acc_in.at[slot], ar_sem.at[slot]).wait()

    barrier = pltpu.get_barrier_semaphore()
    for target in ({"tm": earlier}, {"tm": later}):
        pl.semaphore_signal(barrier, inc=1, device_id=target, device_id_type=MESH)

    @pl.when(me > 0)
    def _():
        pl.semaphore_signal(barrier, inc=1, device_id={"station": me - 1}, device_id_type=MESH)

    @pl.when(me < n - 1)
    def _():
        pl.semaphore_signal(barrier, inc=1, device_id={"station": me + 1}, device_id_type=MESH)

    small = [
        pltpu.make_async_copy(sets_hbm, sets, small_sem.at[0]),
        pltpu.make_async_copy(delays_hbm, delays, small_sem.at[1]),
        pltpu.make_async_copy(taps_hbm, taps, small_sem.at[2]),
    ]
    for copy in small:
        copy.start()

    def load(ch):
        v_copy(ch).start()
        w_copy(ch).start()

    for i in range(LEAD):
        load(ahead_channel(i))

    from_row = lax.broadcasted_iota(jnp.int32, (folds * time_len, time_len), 0)
    to_lane = lax.broadcasted_iota(jnp.int32, (folds * time_len, time_len), 1)
    wanted = (to_lane // pad) * time_len + lax.rem(to_lane, pad) + time_len - pad
    picker = (from_row == wanted).astype(f32).astype(bf16)

    def pack(ch):
        v_copy(ch).wait()
        wide = jnp.concatenate(
            [v_buf[ch, pl.ds(q * fold_rows, fold_rows), :] for q in range(folds)], axis=1
        )
        halo_out[ch] = jnp.dot(wide, picker, preferred_element_type=f32).astype(bf16)
        halo_copy(ch).start()

    present = 2 + jnp.where(me > 0, 1, 0) + jnp.where(me < n - 1, 1, 0)
    pl.semaphore_wait(barrier, present)

    for i in range(LEAD):
        pack(ahead_channel(i))

    for copy in small:
        copy.wait()

    pick_tap = lax.broadcasted_iota(jnp.int32, (tap_count, tap_count * 128), 1) // 128
    tap_row = lax.broadcasted_iota(jnp.int32, (tap_count, tap_count * 128), 0)
    chosen = (pick_tap == tap_row).astype(f32).astype(bf16)
    values = jnp.dot(taps[...], chosen, preferred_element_type=f32)
    for m in range(set_count):
        spread[m] = values[m:m + 1]

    out_pos = lax.broadcasted_iota(jnp.int32, (time_len, 2 * time_len), 0)
    column = lax.broadcasted_iota(jnp.int32, (time_len, 2 * time_len), 1)
    in_pos = jnp.where(column < time_len, column, lax.rem(column, pad) - pad)
    usable = (column < time_len) | (tm > 0)
    lags[...] = jnp.where(usable, out_pos - delays[0] - in_pos, -1)

    def make_band(m, carry):
        lag = lags[...]
        values = jnp.zeros((time_len, 2 * time_len), f32)
        for k in range(tap_count):
            tap = spread[m, :, pl.ds(k * 128, 128)]
            tap = jnp.concatenate([tap] * (2 * time_len // 128), axis=1)
            values = jnp.where(lag == k, tap, values)
        band[m] = values.astype(bf16)
        return carry

    lax.fori_loop(0, set_count, make_band, 0)

    def load_rest(i, carry):
        @pl.when(i < ahead_count)
        def _():
            load(ahead_channel(i))

        j = i - LEAD
        @pl.when(j < back_count)
        def _():
            load(back_channel(j))

        return carry

    lax.fori_loop(LEAD, jnp.maximum(ahead_count, back_count + LEAD), load_rest, 0)

    fold_lane = lax.broadcasted_iota(jnp.int32, (fold_rows, time_len), 1) // pad

    def beams_of(ch):
        halo_copy(ch).wait_recv()
        w_copy(ch).wait()
        rim = halo_in[ch]
        rims = jnp.concatenate(
            [jnp.where(fold_lane == q, rim, jnp.zeros_like(rim)) for q in range(folds)], axis=0
        )
        window = jnp.concatenate([v_buf[ch], rims], axis=1)
        delayed = lax.dot_general(
            band[sets[0, ch]], window, (((1,), (1,)), ((), ())), preferred_element_type=f32
        ).astype(bf16)
        wr = w_buf[ch, pl.ds(0, antennas), :]
        wi = w_buf[ch, pl.ds(antennas, antennas), :]
        steer = jnp.concatenate(
            [jnp.concatenate([wr, wi], axis=1), jnp.concatenate([-wi, wr], axis=1)], axis=0
        )
        return jnp.dot(delayed, steer, preferred_element_type=f32)

    def step(i, carry):
        j = i - offset

        @pl.when(i + LEAD < ahead_count)
        def _():
            pack(ahead_channel(i + LEAD))

        @pl.when((j + LEAD >= 0) & (j + LEAD < back_count))
        def _():
            pack(back_channel(j + LEAD))

        @pl.when(i < ahead_count)
        def _():
            ch = ahead_channel(i)
            total = beams_of(ch)

            @pl.when(place > 0)
            def _():
                wait_arrival(ch)
                acc_out[ch] = (total + acc_in[ch].astype(f32)).astype(bf16)

            @pl.when(place == 0)
            def _():
                acc_out[ch] = total.astype(bf16)

            sum_copy(ch, ahead_dir).start()

        @pl.when((j >= 0) & (j < back_count))
        def _():
            ch = back_channel(j)
            total = beams_of(ch)
            slot = arrival(ch, back_dir)
            wait_arrival(slot)
            total = total + acc_in[slot].astype(f32)

            @pl.when(j < place * rows)
            def _():
                acc_out[ch] = total.astype(bf16)
                sum_copy(ch, back_dir).start()

            @pl.when(j >= place * rows)
            def _():
                own[lax.rem(j, rows)] = total

        return carry

    lax.fori_loop(0, ahead_count + LAG, step, 0)

    def finish(k, carry):
        slot = arrival(me * rows + k, ahead_dir)

        @pl.when(place > 0)
        def _():
            wait_arrival(slot)
            out_buf[k] = (own[k] + acc_in[slot].astype(f32)).T.astype(bf16)

        @pl.when(place == 0)
        def _():
            out_buf[k] = own[k].T.astype(bf16)

        return carry

    lax.fori_loop(0, rows, finish, 0)

    def drain_halo(ch, carry):
        halo_copy(ch).wait_send()
        return carry

    lax.fori_loop(0, channels, drain_halo, 0)

    def drain_ahead(i, carry):
        sum_copy(ahead_channel(i), ahead_dir).wait_send()
        return carry

    lax.fori_loop(0, ahead_count, drain_ahead, 0)

    def drain_back(j, carry):
        sum_copy(back_channel(j), back_dir).wait_send()
        return carry

    lax.fori_loop(0, place * rows, drain_back, 0)


def body(voltages, delays, tap_sets, tap_table, weights):
    _, channels, parts, antennas, time_len = voltages.shape
    beams = weights.shape[-1]
    set_count, tap_count = tap_table.shape
    n = lax.axis_size("station")
    tm_count = lax.axis_size("tm")
    rows = channels // n
    pad = MAXD + tap_count
    rows_in = parts * antennas
    fold_rows = rows_in * pad // time_len
    sizes = (channels, parts, antennas, beams, time_len, pad)
    bf16, f32 = jnp.bfloat16, jnp.float32
    dma = pltpu.SemaphoreType.DMA
    in_hbm = pl.BlockSpec(memory_space=pltpu.HBM)
    result = pl.pallas_call(
        functools.partial(kernel, n, tm_count, sizes),
        out_shape=jax.ShapeDtypeStruct((rows, 2 * beams, time_len), bf16),
        in_specs=[in_hbm] * 5,
        out_specs=pl.BlockSpec(memory_space=pltpu.VMEM),
        scratch_shapes=[
            pltpu.SMEM(tap_sets.shape, jnp.int32),
            pltpu.SMEM(delays.shape, jnp.int32),
            pltpu.VMEM((set_count, tap_count), bf16),
            pltpu.VMEM((set_count, 1, tap_count * 128), f32),
            pltpu.VMEM((time_len, 2 * time_len), jnp.int32),
            pltpu.VMEM((channels, rows_in, time_len), bf16),
            pltpu.VMEM((channels, rows_in, beams), bf16),
            pltpu.VMEM((set_count, time_len, 2 * time_len), bf16),
            pltpu.VMEM((channels, fold_rows, time_len), bf16),
            pltpu.VMEM((channels, fold_rows, time_len), bf16),
            pltpu.VMEM((channels, time_len, 2 * beams), bf16),
            pltpu.VMEM((channels + rows, time_len, 2 * beams), bf16),
            pltpu.VMEM((rows, time_len, 2 * beams), f32),
            dma((3,)),
            dma((channels,)),
            dma((channels,)),
            dma((channels,)),
            dma((channels,)),
            dma((channels,)),
            dma((channels + rows,)),
        ],
        compiler_params=pltpu.CompilerParams(
            collective_id=0, has_side_effects=True, vmem_limit_bytes=60 * 1024 * 1024
        ),
    )(
        tap_sets,
        delays,
        tap_table,
        voltages.reshape(channels, rows_in, time_len),
        weights.reshape(channels, rows_in, beams),
    )
    return result.reshape(rows, 2, beams, time_len)


def solution(mesh):
    return jax.shard_map(
        body,
        mesh=mesh,
        in_specs=(
            P(("group", "station"), "chan", None, None, "tm"),
            P(("group", "station")),
            P(("group", "station"), "chan"),
            P(),
            P(("group", "station"), "chan", None, None, None),
        ),
        out_specs=P(("group", "chan", "station"), None, None, "tm"),
        check_vma=False,
    )
```

time: 90.3 us -> 84.9 us (0.940)
  the two profiles are of different devices: /device:TPU:0 before, /device:TPU:16 now
where the time goes in v1:
time: 84.9 us; the launch traced here: 84.7 us
  Pallas kernels  81.8 us (96%)
  local copies, waits for them, and re-layouts  2.31 us (3%)
    pallas_call x1, Pallas kernels, body(): pl.pallas_call(functools.partial(kernel, n, tm_count, sizes), out_shape=j...  81.8 us
    unnamed x1, local copies, waits for them, and re-layouts  2.31 us

profile of v1, /device:TPU:16, one launch (start us, length us, event | category | flops | bytes accessed | tf_op | source)
XLA Modules:
  0.0 84.7 jit_solution(4154720659324203731)
XLA Ops:
  0.7 81.8 %shard_map.55 = bf16[16,256,128]{2,1,0:T(8,128)(2,1)} custom-call(s32[1,64]{1,0:T(1,128)} %sets_hbm.1, s32[1]{0:T(128)S(6)} %copy.7.delays_hbm, bf16[16,16]{1,0:T(8,128)(2,1)} %taps_hbm.1, bf16[64,192,128]{2,1,0:T(8,128)(2,1)} %bitcast.4, bf16[64,192,128]{2,1,0:T(8,128)(2,1)} %bitcast.5), custom_call_target="tpu_custom_call" | custom-call | tf_op jit(solution)/shard_map/pallas_call | solution.py:291
  82.4 2.3 %copy.8 = bf16[16,2,128,128]{3,2,1,0:T(8,128)(2,1)} copy(bf16[16,2,128,128]{3,2,1,0:T(8,128)(2,1)} %bitcast.3) | data formatting | bytes 2097152

commit v2 on v1

v2 whole, which is shorter than its diff:
```python
import functools

import jax
import jax.numpy as jnp
from jax import lax
from jax.experimental import pallas as pl
from jax.experimental.pallas import tpu as pltpu
from jax.sharding import PartitionSpec as P

MAXD = 16
MESH = pl.DeviceIdType.MESH
LEAD = 4
LAG = 4


def kernel(
    n, tm_count, sizes, sets_hbm, delays_hbm, taps_hbm, v_hbm, w_hbm, out_buf,
    sets, delays, taps, spread, own_lag, rim_lag, v_buf, w_buf, halo_out, halo_in,
    acc_out, acc_in, own,
    small_sem, v_sem, w_sem, hs_sem, hr_sem, as_sem, ar_sem, bs_sem, br_sem,
):
    channels, parts, antennas, beams, time_len, pad, group = sizes
    rows = channels // n
    rows_in = parts * antennas
    folds = time_len // pad
    fold_rows = rows_in // folds
    set_count, tap_count = taps.shape
    head = group if n > 2 else 0
    bf16, f32 = jnp.bfloat16, jnp.float32

    me = lax.axis_index("station")
    tm = lax.axis_index("tm")
    later, earlier = lax.rem(tm + 1, tm_count), lax.rem(tm + tm_count - 1, tm_count)

    flip = jnp.where(me >= n // 2, 1, 0)
    place = me + flip * (n - 1 - 2 * me)
    ahead_dir, back_dir = flip, 1 - flip
    ahead_count = (n - 1 - place) * rows
    back_count = (place + 1) * rows
    offset = LAG + ahead_count - back_count
    start = jnp.where(place == 0, head, 0)

    def channel_of(station, k):
        return (station + flip * (n - 1 - 2 * station)) * rows + k

    def ahead_channel(i):
        return channel_of(n - 1 - i // rows, lax.rem(i, rows))

    def back_channel(j):
        return channel_of(j // rows, lax.rem(j, rows))

    def v_copy(g):
        span = pl.ds(g * group, group)
        return pltpu.make_async_copy(v_hbm.at[span], v_buf.at[span], v_sem.at[g])

    def w_copy(g):
        span = pl.ds(g * group, group)
        return pltpu.make_async_copy(w_hbm.at[span], w_buf.at[span], w_sem.at[g])

    def halo_copy(ch):
        return pltpu.make_async_remote_copy(
            src_ref=halo_out.at[ch],
            dst_ref=halo_in.at[ch],
            send_sem=hs_sem.at[ch],
            recv_sem=hr_sem.at[ch],
            device_id={"tm": later},
            device_id_type=MESH,
        )

    def sum_copy(ch, direction):
        target = me + 1 - 2 * direction
        final = (ch // rows == target) & (direction == 1)
        slot = jnp.where(final, channels + lax.rem(ch, rows), ch)
        return pltpu.make_async_remote_copy(
            src_ref=acc_out.at[ch],
            dst_ref=acc_in.at[slot],
            send_sem=as_sem.at[ch],
            recv_sem=ar_sem.at[slot],
            device_id={"station": target},
            device_id_type=MESH,
        )

    def arrival(ch, direction):
        final = (ch // rows == me) & (direction == 1)
        return jnp.where(final, channels + lax.rem(ch, rows), ch)

    def wait_arrival(slot):
        pltpu.make_async_copy(acc_in.at[slot], acc_in.at[slot], ar_sem.at[slot]).wait()

    late_rows, early_rows = pl.ds(pad, time_len - pad), pl.ds(0, pad)

    def late_copy(i):
        ch = ahead_channel(i)
        return pltpu.make_async_remote_copy(
            src_ref=acc_out.at[ch, late_rows],
            dst_ref=acc_in.at[ch, late_rows],
            send_sem=as_sem.at[ch],
            recv_sem=ar_sem.at[ch],
            device_id={"station": me + 1 - 2 * ahead_dir},
            device_id_type=MESH,
        )

    def early_copy(i):
        ch = ahead_channel(i)
        return pltpu.make_async_remote_copy(
            src_ref=acc_out.at[ch, early_rows],
            dst_ref=acc_in.at[ch, early_rows],
            send_sem=bs_sem.at[i],
            recv_sem=br_sem.at[i],
            device_id={"station": me + 1 - 2 * ahead_dir},
            device_id_type=MESH,
        )

    small = [
        pltpu.make_async_copy(taps_hbm, taps, small_sem.at[0]),
        pltpu.make_async_copy(delays_hbm, delays, small_sem.at[1]),
        pltpu.make_async_copy(sets_hbm, sets, small_sem.at[2]),
    ]
    for copy in small:
        copy.start()
    first_group = ahead_channel(0) // group
    v_copy(first_group).start()
    w_copy(first_group).start()

    barrier = pltpu.get_barrier_semaphore()

    @pl.when(me > 0)
    def _():
        pl.semaphore_signal(barrier, inc=1, device_id={"station": me - 1}, device_id_type=MESH)

    @pl.when(me < n - 1)
    def _():
        pl.semaphore_signal(barrier, inc=1, device_id={"station": me + 1}, device_id_type=MESH)

    for target in ({"tm": earlier}, {"tm": later}):
        pl.semaphore_signal(barrier, inc=1, device_id=target, device_id_type=MESH)

    def load_ahead(g, carry):
        v_copy(ahead_channel(g * group) // group).start()
        w_copy(ahead_channel(g * group) // group).start()
        return carry

    def load_back(g, carry):
        v_copy(back_channel(g * group) // group).start()
        w_copy(back_channel(g * group) // group).start()
        return carry

    lax.fori_loop(1, ahead_count // group, load_ahead, 0)
    lax.fori_loop(0, back_count // group, load_back, 0)

    from_row = lax.broadcasted_iota(jnp.int32, (folds * time_len, time_len), 0)
    to_lane = lax.broadcasted_iota(jnp.int32, (folds * time_len, time_len), 1)
    wanted = (to_lane // pad) * time_len + lax.rem(to_lane, pad) + time_len - pad
    picker = (from_row == wanted).astype(f32).astype(bf16)

    for copy in small:
        copy.wait()

    pick_tap = lax.broadcasted_iota(jnp.int32, (tap_count, tap_count * 128), 1) // 128
    tap_row = lax.broadcasted_iota(jnp.int32, (tap_count, tap_count * 128), 0)
    chosen = (pick_tap == tap_row).astype(f32).astype(bf16)
    values = jnp.dot(taps[...], chosen, preferred_element_type=f32)
    for m in range(set_count):
        spread[m] = values[m:m + 1]

    out_pos = lax.broadcasted_iota(jnp.int32, (time_len, time_len), 0)
    in_pos = lax.broadcasted_iota(jnp.int32, (time_len, time_len), 1)
    own_lag[...] = out_pos - in_pos - delays[0]
    rim_out = lax.broadcasted_iota(jnp.int32, (pad, time_len), 0)
    rim_in = lax.rem(lax.broadcasted_iota(jnp.int32, (pad, time_len), 1), pad) - pad
    rim_lag[...] = jnp.where(tm > 0, rim_out - rim_in - delays[0], -1)

    fold_lane = lax.broadcasted_iota(jnp.int32, (fold_rows, time_len), 1) // pad

    def toeplitz(m, lag):
        values = jnp.zeros(lag.shape, f32)
        for k in range(tap_count):
            values = jnp.where(lag == k, spread[m, :, pl.ds(k * 128, 128)], values)
        return values.astype(bf16)

    def rims_of(ch):
        rim = halo_in[ch]
        return jnp.concatenate(
            [jnp.where(fold_lane == q, rim, jnp.zeros_like(rim)) for q in range(folds)], axis=0
        )

    def filtered(filt, window):
        return lax.dot_general(
            filt, window, (((1,), (1,)), ((), ())), preferred_element_type=f32
        ).astype(bf16)

    def steered(ch, delayed):
        wr = w_buf[ch, pl.ds(0, antennas), :]
        wi = w_buf[ch, pl.ds(antennas, antennas), :]
        steer = jnp.concatenate(
            [jnp.concatenate([wr, wi], axis=1), jnp.concatenate([-wi, wr], axis=1)], axis=0
        )
        return jnp.dot(delayed, steer, preferred_element_type=f32)

    def beams_of(ch):
        halo_copy(ch).wait_recv()
        m = sets[0, ch]
        rim = toeplitz(m, rim_lag[...])
        rim = jnp.concatenate([rim, jnp.zeros((time_len - pad, time_len), bf16)], axis=0)
        filt = jnp.concatenate([toeplitz(m, own_lag[...]), rim], axis=1)
        window = jnp.concatenate([v_buf[ch], rims_of(ch)], axis=1)
        return steered(ch, filtered(filt, window))

    def pack(ch):
        wide = jnp.concatenate(
            [v_buf[ch, pl.ds(q * fold_rows, fold_rows), :] for q in range(folds)], axis=1
        )
        halo_out[ch] = jnp.dot(wide, picker, preferred_element_type=f32).astype(bf16)
        halo_copy(ch).start()

    def pack_ahead(i):
        ch = ahead_channel(i)

        @pl.when(lax.rem(i, group) == 0)
        def _():
            v_copy(ch // group).wait()

        pack(ch)

    def pack_back(j):
        ch = back_channel(j)

        @pl.when(lax.rem(j, group) == 0)
        def _():
            v_copy(ch // group).wait()

        pack(ch)

    present = 2 + jnp.where(me > 0, 1, 0) + jnp.where(me < n - 1, 1, 0)
    pl.semaphore_wait(barrier, present)

    if head:
        @pl.when(place == 0)
        def _():
            v_copy(first_group).wait()
            w_copy(first_group).wait()

            def send_late(i, carry):
                ch = ahead_channel(i)
                filt = toeplitz(sets[0, ch], own_lag[late_rows, :])
                total = steered(ch, filtered(filt, v_buf[ch]))
                acc_out[ch, late_rows, :] = total.astype(bf16)
                late_copy(i).start()
                return carry

            lax.fori_loop(0, head, send_late, 0)

            def pack_head(i, carry):
                pack(ahead_channel(i))
                return carry

            lax.fori_loop(0, head, pack_head, 0)

    def pack_first(i, carry):
        pack_ahead(i)
        return carry

    lax.fori_loop(start, start + LEAD, pack_first, 0)

    if head:
        @pl.when(place == 0)
        def _():
            def send_early(i, carry):
                ch = ahead_channel(i)
                halo_copy(ch).wait_recv()
                m = sets[0, ch]
                filt = jnp.concatenate(
                    [toeplitz(m, own_lag[early_rows, :]), toeplitz(m, rim_lag[...])], axis=1
                )
                window = jnp.concatenate([v_buf[ch], rims_of(ch)], axis=1)
                total = steered(ch, filtered(filt, window))
                acc_out[ch, early_rows, :] = total.astype(bf16)
                early_copy(i).start()
                return carry

            lax.fori_loop(0, head, send_early, 0)

    def step(i, carry):
        j = i - offset

        @pl.when(i + LEAD < ahead_count)
        def _():
            pack_ahead(i + LEAD)

        @pl.when((j + LEAD >= 0) & (j + LEAD < back_count))
        def _():
            pack_back(j + LEAD)

        @pl.when(i < ahead_count)
        def _():
            ch = ahead_channel(i)

            @pl.when(lax.rem(i, group) == 0)
            def _():
                w_copy(ch // group).wait()

            total = beams_of(ch)

            @pl.when(place > 0)
            def _():
                cut = (place == 1) & (i < head)

                if head:
                    @pl.when(cut)
                    def _():
                        late_copy(i).wait_recv()
                        early_copy(jnp.where(cut, i, 0)).wait_recv()

                @pl.when(jnp.logical_not(cut))
                def _():
                    wait_arrival(ch)

                acc_out[ch] = (total + acc_in[ch].astype(f32)).astype(bf16)

            @pl.when(place == 0)
            def _():
                acc_out[ch] = total.astype(bf16)

            sum_copy(ch, ahead_dir).start()

        @pl.when((j >= 0) & (j < back_count))
        def _():
            ch = back_channel(j)

            @pl.when(lax.rem(j, group) == 0)
            def _():
                w_copy(ch // group).wait()

            total = beams_of(ch)
            slot = arrival(ch, back_dir)
            wait_arrival(slot)
            total = total + acc_in[slot].astype(f32)

            @pl.when(j < place * rows)
            def _():
                acc_out[ch] = total.astype(bf16)
                sum_copy(ch, back_dir).start()

            @pl.when(j >= place * rows)
            def _():
                own[lax.rem(j, rows)] = total

        return carry

    lax.fori_loop(start, ahead_count + LAG, step, 0)

    def drain_halo(ch, carry):
        halo_copy(ch).wait_send()
        return carry

    lax.fori_loop(0, channels, drain_halo, 0)

    def drain_back(j, carry):
        sum_copy(back_channel(j), back_dir).wait_send()
        return carry

    lax.fori_loop(0, place * rows, drain_back, 0)

    def drain_ahead(i, carry):
        sum_copy(ahead_channel(i), ahead_dir).wait_send()
        return carry

    @pl.when(place > 0)
    def _():
        lax.fori_loop(0, ahead_count, drain_ahead, 0)

        def finish(k, carry):
            slot = arrival(me * rows + k, ahead_dir)
            wait_arrival(slot)
            out_buf[k] = (own[k] + acc_in[slot].astype(f32)).T.astype(bf16)
            return carry

        lax.fori_loop(0, rows, finish, 0)

    @pl.when(place == 0)
    def _():
        def finish(k, carry):
            out_buf[k] = own[k].T.astype(bf16)
            return carry

        lax.fori_loop(0, rows, finish, 0)

        if head:
            def drain_head(i, carry):
                late_copy(i).wait_send()
                early_copy(i).wait_send()
                return carry

            lax.fori_loop(0, head, drain_head, 0)

        lax.fori_loop(head, ahead_count, drain_ahead, 0)


def body(voltages, delays, tap_sets, tap_table, weights):
    _, channels, parts, antennas, time_len = voltages.shape
    beams = weights.shape[-1]
    set_count, tap_count = tap_table.shape
    n = lax.axis_size("station")
    tm_count = lax.axis_size("tm")
    rows = channels // n
    pad = MAXD + tap_count
    rows_in = parts * antennas
    fold_rows = rows_in * pad // time_len
    group = max(rows // 4, 1)
    groups = channels // group
    sizes = (channels, parts, antennas, beams, time_len, pad, group)
    bf16, f32 = jnp.bfloat16, jnp.float32
    dma = pltpu.SemaphoreType.DMA
    in_hbm = pl.BlockSpec(memory_space=pltpu.HBM)
    operands = (
        tap_sets,
        delays,
        tap_table,
        voltages.reshape(channels, rows_in, time_len),
        weights.reshape(channels, rows_in, beams),
    )
    result = pl.pallas_call(
        functools.partial(kernel, n, tm_count, sizes),
        out_shape=pltpu.VMEM((rows, 2 * beams, time_len), bf16),
        in_specs=[in_hbm] * 5,
        out_specs=pl.BlockSpec(memory_space=pltpu.VMEM),
        scratch_shapes=[
            pltpu.SMEM(tap_sets.shape, jnp.int32),
            pltpu.SMEM(delays.shape, jnp.int32),
            pltpu.VMEM((set_count, tap_count), bf16),
            pltpu.VMEM((set_count, 1, tap_count * 128), f32),
            pltpu.VMEM((time_len, time_len), jnp.int32),
            pltpu.VMEM((pad, time_len), jnp.int32),
            pltpu.VMEM((channels, rows_in, time_len), bf16),
            pltpu.VMEM((channels, rows_in, beams), bf16),
            pltpu.VMEM((channels, fold_rows, time_len), bf16),
            pltpu.VMEM((channels, fold_rows, time_len), bf16),
            pltpu.VMEM((channels, time_len, 2 * beams), bf16),
            pltpu.VMEM((channels + rows, time_len, 2 * beams), bf16),
            pltpu.VMEM((rows, time_len, 2 * beams), f32),
            dma((3,)),
            dma((groups,)),
            dma((groups,)),
            dma((channels,)),
            dma((channels,)),
            dma((channels,)),
            dma((channels + rows,)),
            dma((group,)),
            dma((group,)),
        ],
        compiler_params=pltpu.CompilerParams(
            collective_id=0, has_side_effects=True, vmem_limit_bytes=40 * 1024 * 1024
        ),
    )(*(x if x.ndim == 1 else pltpu.with_memory_space_constraint(x, pltpu.HBM) for x in operands))
    return result.reshape(rows, 2, beams, time_len)


def solution(mesh):
    return jax.shard_map(
        body,
        mesh=mesh,
        in_specs=(
            P(("group", "station"), "chan", None, None, "tm"),
            P(("group", "station")),
            P(("group", "station"), "chan"),
            P(),
            P(("group", "station"), "chan", None, None, None),
        ),
        out_specs=P(("group", "chan", "station"), None, None, "tm"),
        check_vma=False,
    )
```

time: 84.9 us -> 76 us (0.90)
  Pallas kernels: 81.8 us -> 74.2 us
  local copies, waits for them, and re-layouts: 2.31 us -> 0.97 us
    pallas_call x1, Pallas kernels: 81.8 us -> 74.2 us  [body(): pl.pallas_call(functools.partial(kernel, n, tm_count, sizes), out_shape=p...]
    unnamed x1, local copies, waits for them, and re-layouts: 2.31 us -> 0.97 us
where the time goes in v2:
time: 76 us; the launch traced here: 75.9 us
  Pallas kernels  74.2 us (98%)
  local copies, waits for them, and re-layouts  0.97 us (1%)
    pallas_call x1, Pallas kernels, body(): pl.pallas_call(functools.partial(kernel, n, tm_count, sizes), out_shape=p...  74.2 us

profile of v2, /device:TPU:16, one launch (start us, length us, event | category | flops | bytes accessed | tf_op | source)
XLA Modules:
  0.0 75.9 jit_solution(6547119882650378161)
XLA Ops:
  0.7 74.2 %shard_map.55 = bf16[16,256,128]{2,1,0:T(8,128)(2,1)S(1)} custom-call(s32[1,64]{1,0:T(1,128)} %sets_hbm.1, s32[1]{0:T(128)S(6)} %copy.8.delays_hbm, bf16[16,16]{1,0:T(8,128)(2,1)} %taps_hbm.1, bf16[64,192,128]{2,1,0:T(8,128)(2,1)} %bitcast.4, bf16[64,192,128]{2,1,0:T(8,128)(2,1)} %bitcast.5), custom_call_target="tpu_custom_call" | custom-call | tf_op jit(solution)/shard_map/pallas_call | solution.py:422
  74.9 1.0 %copy.7 = bf16[16,2,128,128]{3,2,1,0:T(8,128)(2,1)} copy(bf16[16,2,128,128]{3,2,1,0:T(8,128)(2,1)S(1)} %bitcast.3) | data formatting | bytes 2097152

commit v3 on v2

--- a/solution.py
+++ b/solution.py
@@ -9,15 +9,15 @@
 
 MAXD = 16
 MESH = pl.DeviceIdType.MESH
-LEAD = 4
-LAG = 4
+LEAD = 8
+LAG = 12
 
 
 def kernel(
     n, tm_count, sizes, sets_hbm, delays_hbm, taps_hbm, v_hbm, w_hbm, out_buf,
     sets, delays, taps, spread, own_lag, rim_lag, v_buf, w_buf, halo_out, halo_in,
     acc_out, acc_in, own,
-    small_sem, v_sem, w_sem, hs_sem, hr_sem, as_sem, ar_sem, bs_sem, br_sem,
+    small_sem, load_sem, hs_sem, hr_sem, as_sem, ar_sem,
 ):
     channels, parts, antennas, beams, time_len, pad, group = sizes
     rows = channels // n
@@ -39,6 +39,8 @@
     back_count = (place + 1) * rows
     offset = LAG + ahead_count - back_count
     start = jnp.where(place == 0, head, 0)
+    single_from = jnp.where(place < n // 2 - 1, ahead_count - group, ahead_count)
+    shared = (channels + rows) // group
 
     def channel_of(station, k):
         return (station + flip * (n - 1 - 2 * station)) * rows + k
@@ -49,33 +51,33 @@
     def back_channel(j):
         return channel_of(j // rows, lax.rem(j, rows))
 
-    def v_copy(g):
-        span = pl.ds(g * group, group)
-        return pltpu.make_async_copy(v_hbm.at[span], v_buf.at[span], v_sem.at[g])
-
-    def w_copy(g):
-        span = pl.ds(g * group, group)
-        return pltpu.make_async_copy(w_hbm.at[span], w_buf.at[span], w_sem.at[g])
+    def load(first, count, sems):
+        span = pl.ds(first, count)
+        return (
+            pltpu.make_async_copy(v_hbm.at[span], v_buf.at[span], load_sem.at[sems]),
+            pltpu.make_async_copy(w_hbm.at[span], w_buf.at[span], load_sem.at[sems + 1]),
+        )
 
     def halo_copy(ch):
+        span = pl.ds(ch, group)
         return pltpu.make_async_remote_copy(
-            src_ref=halo_out.at[ch],
-            dst_ref=halo_in.at[ch],
-            send_sem=hs_sem.at[ch],
-            recv_sem=hr_sem.at[ch],
+            src_ref=halo_out.at[span],
+            dst_ref=halo_in.at[span],
+            send_sem=hs_sem,
+            recv_sem=hr_sem.at[ch // group],
             device_id={"tm": later},
             device_id_type=MESH,
         )
 
-    def sum_copy(ch, direction):
+    def sum_copy(ch, direction, single=False):
         target = me + 1 - 2 * direction
         final = (ch // rows == target) & (direction == 1)
         slot = jnp.where(final, channels + lax.rem(ch, rows), ch)
         return pltpu.make_async_remote_copy(
             src_ref=acc_out.at[ch],
             dst_ref=acc_in.at[slot],
-            send_sem=as_sem.at[ch],
-            recv_sem=ar_sem.at[slot],
+            send_sem=as_sem,
+            recv_sem=ar_sem.at[jnp.where(single, shared + lax.rem(ch, group), slot // group)],
             device_id={"station": target},
             device_id_type=MESH,
         )
@@ -84,29 +86,23 @@
         final = (ch // rows == me) & (direction == 1)
         return jnp.where(final, channels + lax.rem(ch, rows), ch)
 
-    def wait_arrival(slot):
-        pltpu.make_async_copy(acc_in.at[slot], acc_in.at[slot], ar_sem.at[slot]).wait()
+    def wait_group(slot):
+        span = acc_in.at[pl.ds(slot, group)]
+        pltpu.make_async_copy(span, span, ar_sem.at[slot // group]).wait()
+
+    def wait_single(slot):
+        sem = ar_sem.at[shared + lax.rem(slot, group)]
+        pltpu.make_async_copy(acc_in.at[slot], acc_in.at[slot], sem).wait()
 
     late_rows, early_rows = pl.ds(pad, time_len - pad), pl.ds(0, pad)
 
-    def late_copy(i):
+    def piece_copy(i, piece):
         ch = ahead_channel(i)
         return pltpu.make_async_remote_copy(
-            src_ref=acc_out.at[ch, late_rows],
-            dst_ref=acc_in.at[ch, late_rows],
-            send_sem=as_sem.at[ch],
-            recv_sem=ar_sem.at[ch],
-            device_id={"station": me + 1 - 2 * ahead_dir},
-            device_id_type=MESH,
-        )
-
-    def early_copy(i):
-        ch = ahead_channel(i)
-        return pltpu.make_async_remote_copy(
-            src_ref=acc_out.at[ch, early_rows],
-            dst_ref=acc_in.at[ch, early_rows],
-            send_sem=bs_sem.at[i],
-            recv_sem=br_sem.at[i],
+            src_ref=acc_out.at[ch, piece],
+            dst_ref=acc_in.at[ch, piece],
+            send_sem=as_sem,
+            recv_sem=ar_sem.at[ch // group],
             device_id={"station": me + 1 - 2 * ahead_dir},
             device_id_type=MESH,
         )
@@ -116,11 +112,12 @@
         pltpu.make_async_copy(delays_hbm, delays, small_sem.at[1]),
         pltpu.make_async_copy(sets_hbm, sets, small_sem.at[2]),
     ]
+    first = ahead_channel(0)
+    first_loads = load(first, group, 0)
+    for copy in first_loads:
+        copy.start()
     for copy in small:
         copy.start()
-    first_group = ahead_channel(0) // group
-    v_copy(first_group).start()
-    w_copy(first_group).start()
 
     barrier = pltpu.get_barrier_semaphore()
 
@@ -135,18 +132,15 @@
     for target in ({"tm": earlier}, {"tm": later}):
         pl.semaphore_signal(barrier, inc=1, device_id=target, device_id_type=MESH)
 
-    def load_ahead(g, carry):
-        v_copy(ahead_channel(g * group) // group).start()
-        w_copy(ahead_channel(g * group) // group).start()
+    for copy in load(first + group, rows - group, 2):
+        copy.start()
+
+    def load_rest(station, carry):
+        for copy in load(channel_of(station, 0), rows, 2):
+            copy.start()
         return carry
 
-    def load_back(g, carry):
-        v_copy(back_channel(g * group) // group).start()
-        w_copy(back_channel(g * group) // group).start()
-        return carry
-
-    lax.fori_loop(1, ahead_count // group, load_ahead, 0)
-    lax.fori_loop(0, back_count // group, load_back, 0)
+    lax.fori_loop(0, n - 1, load_rest, 0)
 
     from_row = lax.broadcasted_iota(jnp.int32, (folds * time_len, time_len), 0)
     to_lane = lax.broadcasted_iota(jnp.int32, (folds * time_len, time_len), 1)
@@ -198,7 +192,10 @@
         return jnp.dot(delayed, steer, preferred_element_type=f32)
 
     def beams_of(ch):
-        halo_copy(ch).wait_recv()
+        @pl.when(lax.rem(ch, group) == 0)
+        def _():
+            halo_copy(ch).wait_recv()
+
         m = sets[0, ch]
         rim = toeplitz(m, rim_lag[...])
         rim = jnp.concatenate([rim, jnp.zeros((time_len - pad, time_len), bf16)], axis=0)
@@ -211,25 +208,24 @@
             [v_buf[ch, pl.ds(q * fold_rows, fold_rows), :] for q in range(folds)], axis=1
         )
         halo_out[ch] = jnp.dot(wide, picker, preferred_element_type=f32).astype(bf16)
-        halo_copy(ch).start()
-
-    def pack_ahead(i):
+
+        @pl.when(lax.rem(ch, group) == group - 1)
+        def _():
+            halo_copy(ch - (group - 1)).start()
+
+    def late_rows_of(i):
         ch = ahead_channel(i)
-
-        @pl.when(lax.rem(i, group) == 0)
-        def _():
-            v_copy(ch // group).wait()
-
-        pack(ch)
-
-    def pack_back(j):
-        ch = back_channel(j)
-
-        @pl.when(lax.rem(j, group) == 0)
-        def _():
-            v_copy(ch // group).wait()
-
-        pack(ch)
+        filt = toeplitz(sets[0, ch], own_lag[late_rows, :])
+        total = steered(ch, filtered(filt, v_buf[ch]))
+        acc_out[ch, late_rows, :] = total.astype(bf16)
+
+    for copy in first_loads:
+        copy.wait()
+
+    if head:
+        @pl.when(place == 0)
+        def _():
+            late_rows_of(0)
 
     present = 2 + jnp.where(me > 0, 1, 0) + jnp.where(me < n - 1, 1, 0)
     pl.semaphore_wait(barrier, present)
@@ -237,18 +233,14 @@
     if head:
         @pl.when(place == 0)
         def _():
-            v_copy(first_group).wait()
-            w_copy(first_group).wait()
+            piece_copy(0, late_rows).start()
 
             def send_late(i, carry):
-                ch = ahead_channel(i)
-                filt = toeplitz(sets[0, ch], own_lag[late_rows, :])
-                total = steered(ch, filtered(filt, v_buf[ch]))
-                acc_out[ch, late_rows, :] = total.astype(bf16)
-                late_copy(i).start()
+                late_rows_of(i)
+                piece_copy(i, late_rows).start()
                 return carry
 
-            lax.fori_loop(0, head, send_late, 0)
+            lax.fori_loop(1, head, send_late, 0)
 
             def pack_head(i, carry):
                 pack(ahead_channel(i))
@@ -256,8 +248,11 @@
 
             lax.fori_loop(0, head, pack_head, 0)
 
+    for copy in load(0, channels - group, 2):
+        copy.wait()
+
     def pack_first(i, carry):
-        pack_ahead(i)
+        pack(ahead_channel(i))
         return carry
 
     lax.fori_loop(start, start + LEAD, pack_first, 0)
@@ -267,7 +262,11 @@
         def _():
             def send_early(i, carry):
                 ch = ahead_channel(i)
-                halo_copy(ch).wait_recv()
+
+                @pl.when(i == 0)
+                def _():
+                    halo_copy(ch).wait_recv()
+
                 m = sets[0, ch]
                 filt = jnp.concatenate(
                     [toeplitz(m, own_lag[early_rows, :]), toeplitz(m, rim_lag[...])], axis=1
@@ -275,7 +274,7 @@
                 window = jnp.concatenate([v_buf[ch], rims_of(ch)], axis=1)
                 total = steered(ch, filtered(filt, window))
                 acc_out[ch, early_rows, :] = total.astype(bf16)
-                early_copy(i).start()
+                piece_copy(i, early_rows).start()
                 return carry
 
             lax.fori_loop(0, head, send_early, 0)
@@ -285,35 +284,22 @@
 
         @pl.when(i + LEAD < ahead_count)
         def _():
-            pack_ahead(i + LEAD)
+            pack(ahead_channel(i + LEAD))
 
         @pl.when((j + LEAD >= 0) & (j + LEAD < back_count))
         def _():
-            pack_back(j + LEAD)
+            pack(back_channel(j + LEAD))
 
         @pl.when(i < ahead_count)
         def _():
             ch = ahead_channel(i)
-
-            @pl.when(lax.rem(i, group) == 0)
-            def _():
-                w_copy(ch // group).wait()
-
             total = beams_of(ch)
 
             @pl.when(place > 0)
             def _():
-                cut = (place == 1) & (i < head)
-
-                if head:
-                    @pl.when(cut)
-                    def _():
-                        late_copy(i).wait_recv()
-                        early_copy(jnp.where(cut, i, 0)).wait_recv()
-
-                @pl.when(jnp.logical_not(cut))
+                @pl.when(lax.rem(i, group) == 0)
                 def _():
-                    wait_arrival(ch)
+                    wait_group(ch)
 
                 acc_out[ch] = (total + acc_in[ch].astype(f32)).astype(bf16)
 
@@ -321,19 +307,18 @@
             def _():
                 acc_out[ch] = total.astype(bf16)
 
-            sum_copy(ch, ahead_dir).start()
+            sum_copy(ch, ahead_dir, i >= single_from).start()
 
         @pl.when((j >= 0) & (j < back_count))
         def _():
             ch = back_channel(j)
-
-            @pl.when(lax.rem(j, group) == 0)
-            def _():
-                w_copy(ch // group).wait()
-
             total = beams_of(ch)
             slot = arrival(ch, back_dir)
-            wait_arrival(slot)
+
+            @pl.when(lax.rem(j, group) == 0)
+            def _():
+                wait_group(slot)
+
             total = total + acc_in[slot].astype(f32)
 
             @pl.when(j < place * rows)
@@ -349,29 +334,41 @@
 
     lax.fori_loop(start, ahead_count + LAG, step, 0)
 
-    def drain_halo(ch, carry):
-        halo_copy(ch).wait_send()
-        return carry
-
-    lax.fori_loop(0, channels, drain_halo, 0)
-
-    def drain_back(j, carry):
-        sum_copy(back_channel(j), back_dir).wait_send()
-        return carry
-
-    lax.fori_loop(0, place * rows, drain_back, 0)
-
-    def drain_ahead(i, carry):
-        sum_copy(ahead_channel(i), ahead_dir).wait_send()
-        return carry
+    def drain():
+        pltpu.make_async_remote_copy(
+            src_ref=halo_out,
+            dst_ref=halo_in,
+            send_sem=hs_sem,
+            recv_sem=hr_sem.at[0],
+            device_id={"tm": later},
+            device_id_type=MESH,
+        ).wait_send()
+        sent = pl.ds(0, (n - 1) * rows)
+        pltpu.make_async_remote_copy(
+            src_ref=acc_out.at[sent],
+            dst_ref=acc_in.at[sent],
+            send_sem=as_sem,
+            recv_sem=ar_sem.at[0],
+            device_id={"tm": later},
+            device_id_type=MESH,
+        ).wait_send()
 
     @pl.when(place > 0)
     def _():
-        lax.fori_loop(0, ahead_count, drain_ahead, 0)
+        drain()
 
         def finish(k, carry):
             slot = arrival(me * rows + k, ahead_dir)
-            wait_arrival(slot)
+            single = k >= rows - group
+
+            @pl.when(single)
+            def _():
+                wait_single(slot)
+
+            @pl.when(jnp.logical_not(single) & (lax.rem(k, group) == 0))
+            def _():
+                wait_group(slot)
+
             out_buf[k] = (own[k] + acc_in[slot].astype(f32)).T.astype(bf16)
             return carry
 
@@ -384,16 +381,7 @@
             return carry
 
         lax.fori_loop(0, rows, finish, 0)
-
-        if head:
-            def drain_head(i, carry):
-                late_copy(i).wait_send()
-                early_copy(i).wait_send()
-                return carry
-
-            lax.fori_loop(0, head, drain_head, 0)
-
-        lax.fori_loop(head, ahead_count, drain_ahead, 0)
+        drain()
 
 
 def body(voltages, delays, tap_sets, tap_table, weights):
@@ -407,7 +395,6 @@
     rows_in = parts * antennas
     fold_rows = rows_in * pad // time_len
     group = max(rows // 4, 1)
-    groups = channels // group
     sizes = (channels, parts, antennas, beams, time_len, pad, group)
     bf16, f32 = jnp.bfloat16, jnp.float32
     dma = pltpu.SemaphoreType.DMA
@@ -439,14 +426,11 @@
             pltpu.VMEM((channels + rows, time_len, 2 * beams), bf16),
             pltpu.VMEM((rows, time_len, 2 * beams), f32),
             dma((3,)),
-            dma((groups,)),
-            dma((groups,)),
-            dma((channels,)),
-            dma((channels,)),
-            dma((channels,)),
-            dma((channels + rows,)),
-            dma((group,)),
-            dma((group,)),
+            dma((4,)),
+            dma(()),
+            dma((channels // group,)),
+            dma(()),
+            dma(((channels + rows) // group + group,)),
         ],
         compiler_params=pltpu.CompilerParams(
             collective_id=0, has_side_effects=True, vmem_limit_bytes=40 * 1024 * 1024

time: 76 us -> 74.4 us (0.979)
  Pallas kernels: 74.2 us -> 72.6 us
    pallas_call x1, Pallas kernels: 74.2 us -> 72.6 us  [body(): pl.pallas_call(functools.partial(kernel, n, tm_count, sizes), out_shape=p...]
where the time goes in v3:
time: 74.4 us; the launch traced here: 74.2 us
  Pallas kernels  72.6 us (98%)
  local copies, waits for them, and re-layouts  0.97 us (1%)
    pallas_call x1, Pallas kernels, body(): pl.pallas_call(functools.partial(kernel, n, tm_count, sizes), out_shape=p...  72.6 us

profile of v3, /device:TPU:16, one launch (start us, length us, event | category | flops | bytes accessed | tf_op | source)
XLA Modules:
  0.0 74.2 jit_solution(5075405234912879348)
XLA Ops:
  0.7 72.6 %shard_map.55 = bf16[16,256,128]{2,1,0:T(8,128)(2,1)S(1)} custom-call(s32[1,64]{1,0:T(1,128)} %sets_hbm.1, s32[1]{0:T(128)S(6)} %copy.8.delays_hbm, bf16[16,16]{1,0:T(8,128)(2,1)} %taps_hbm.1, bf16[64,192,128]{2,1,0:T(8,128)(2,1)} %bitcast.4, bf16[64,192,128]{2,1,0:T(8,128)(2,1)} %bitcast.5), custom_call_target="tpu_custom_call" | custom-call | tf_op jit(solution)/shard_map/pallas_call | solution.py:409
  73.3 1.0 %copy.7 = bf16[16,2,128,128]{3,2,1,0:T(8,128)(2,1)} copy(bf16[16,2,128,128]{3,2,1,0:T(8,128)(2,1)S(1)} %bitcast.3) | data formatting | bytes 2097152

commit v4 on v3

--- a/solution.py
+++ b/solution.py
@@ -9,7 +9,7 @@
 
 MAXD = 16
 MESH = pl.DeviceIdType.MESH
-LEAD = 8
+LEAD = 12
 LAG = 12
 
 
@@ -25,7 +25,7 @@
     folds = time_len // pad
     fold_rows = rows_in // folds
     set_count, tap_count = taps.shape
-    head = group if n > 2 else 0
+    head = 2 * group if n > 2 else 0
     bf16, f32 = jnp.bfloat16, jnp.float32
 
     me = lax.axis_index("station")
@@ -113,7 +113,7 @@
         pltpu.make_async_copy(sets_hbm, sets, small_sem.at[2]),
     ]
     first = ahead_channel(0)
-    first_loads = load(first, group, 0)
+    first_loads = load(first, max(head, group), 0)
     for copy in first_loads:
         copy.start()
     for copy in small:
@@ -132,7 +132,7 @@
     for target in ({"tm": earlier}, {"tm": later}):
         pl.semaphore_signal(barrier, inc=1, device_id=target, device_id_type=MESH)
 
-    for copy in load(first + group, rows - group, 2):
+    for copy in load(first + max(head, group), rows - max(head, group), 2):
         copy.start()
 
     def load_rest(station, carry):
@@ -248,7 +248,7 @@
 
             lax.fori_loop(0, head, pack_head, 0)
 
-    for copy in load(0, channels - group, 2):
+    for copy in load(0, channels - max(head, group), 2):
         copy.wait()
 
     def pack_first(i, carry):
@@ -263,7 +263,7 @@
             def send_early(i, carry):
                 ch = ahead_channel(i)
 
-                @pl.when(i == 0)
+                @pl.when(lax.rem(i, group) == 0)
                 def _():
                     halo_copy(ch).wait_recv()
 

time: 74.4 us -> 73.5 us (0.988)
  Pallas kernels: 72.6 us -> 71.7 us
    pallas_call x1, Pallas kernels: 72.6 us -> 71.7 us  [body(): pl.pallas_call(functools.partial(kernel, n, tm_count, sizes), out_shape=p...]
where the time goes in v4:
time: 73.5 us; the launch traced here: 73.3 us
  Pallas kernels  71.7 us (98%)
  local copies, waits for them, and re-layouts  0.97 us (1%)
    pallas_call x1, Pallas kernels, body(): pl.pallas_call(functools.partial(kernel, n, tm_count, sizes), out_shape=p...  71.7 us

profile of v4, /device:TPU:16, one launch (start us, length us, event | category | flops | bytes accessed | tf_op | source)
XLA Modules:
  0.0 73.3 jit_solution(7960133113918753157)
XLA Ops:
  0.7 71.7 %shard_map.55 = bf16[16,256,128]{2,1,0:T(8,128)(2,1)S(1)} custom-call(s32[1,64]{1,0:T(1,128)} %sets_hbm.1, s32[1]{0:T(128)S(6)} %copy.8.delays_hbm, bf16[16,16]{1,0:T(8,128)(2,1)} %taps_hbm.1, bf16[64,192,128]{2,1,0:T(8,128)(2,1)} %bitcast.4, bf16[64,192,128]{2,1,0:T(8,128)(2,1)} %bitcast.5), custom_call_target="tpu_custom_call" | custom-call | tf_op jit(solution)/shard_map/pallas_call | solution.py:409
  72.3 1.0 %copy.7 = bf16[16,2,128,128]{3,2,1,0:T(8,128)(2,1)} copy(bf16[16,2,128,128]{3,2,1,0:T(8,128)(2,1)S(1)} %bitcast.3) | data formatting | bytes 2097152

commit v5 on v4

--- a/solution.py
+++ b/solution.py
@@ -9,8 +9,8 @@
 
 MAXD = 16
 MESH = pl.DeviceIdType.MESH
-LEAD = 12
-LAG = 12
+LEAD = 16
+LAG = 16
 
 
 def kernel(
@@ -25,7 +25,8 @@
     folds = time_len // pad
     fold_rows = rows_in // folds
     set_count, tap_count = taps.shape
-    head = 2 * group if n > 2 else 0
+    head = group if n > 2 else 0
+    tail = max(group // 2, 1)
     bf16, f32 = jnp.bfloat16, jnp.float32
 
     me = lax.axis_index("station")
@@ -39,7 +40,7 @@
     back_count = (place + 1) * rows
     offset = LAG + ahead_count - back_count
     start = jnp.where(place == 0, head, 0)
-    single_from = jnp.where(place < n // 2 - 1, ahead_count - group, ahead_count)
+    single_from = jnp.where(place < n // 2 - 1, ahead_count - tail, ahead_count)
     shared = (channels + rows) // group
 
     def channel_of(station, k):
@@ -77,7 +78,7 @@
             src_ref=acc_out.at[ch],
             dst_ref=acc_in.at[slot],
             send_sem=as_sem,
-            recv_sem=ar_sem.at[jnp.where(single, shared + lax.rem(ch, group), slot // group)],
+            recv_sem=ar_sem.at[jnp.where(single, shared + lax.rem(ch, tail), slot // group)],
             device_id={"station": target},
             device_id_type=MESH,
         )
@@ -86,12 +87,12 @@
         final = (ch // rows == me) & (direction == 1)
         return jnp.where(final, channels + lax.rem(ch, rows), ch)
 
-    def wait_group(slot):
-        span = acc_in.at[pl.ds(slot, group)]
+    def wait_group(slot, count=group):
+        span = acc_in.at[pl.ds(slot, count)]
         pltpu.make_async_copy(span, span, ar_sem.at[slot // group]).wait()
 
     def wait_single(slot):
-        sem = ar_sem.at[shared + lax.rem(slot, group)]
+        sem = ar_sem.at[shared + lax.rem(slot, tail)]
         pltpu.make_async_copy(acc_in.at[slot], acc_in.at[slot], sem).wait()
 
     late_rows, early_rows = pl.ds(pad, time_len - pad), pl.ds(0, pad)
@@ -359,15 +360,18 @@
 
         def finish(k, carry):
             slot = arrival(me * rows + k, ahead_dir)
-            single = k >= rows - group
-
-            @pl.when(single)
+            @pl.when(k >= rows - tail)
             def _():
                 wait_single(slot)
 
-            @pl.when(jnp.logical_not(single) & (lax.rem(k, group) == 0))
+            @pl.when((k < rows - group) & (lax.rem(k, group) == 0))
             def _():
                 wait_group(slot)
+
+            if group > tail:
+                @pl.when(k == rows - group)
+                def _():
+                    wait_group(slot, group - tail)
 
             out_buf[k] = (own[k] + acc_in[slot].astype(f32)).T.astype(bf16)
             return carry
@@ -394,7 +398,7 @@
     pad = MAXD + tap_count
     rows_in = parts * antennas
     fold_rows = rows_in * pad // time_len
-    group = max(rows // 4, 1)
+    group = max(rows // 2, 1)
     sizes = (channels, parts, antennas, beams, time_len, pad, group)
     bf16, f32 = jnp.bfloat16, jnp.float32
     dma = pltpu.SemaphoreType.DMA
@@ -430,7 +434,7 @@
             dma(()),
             dma((channels // group,)),
             dma(()),
-            dma(((channels + rows) // group + group,)),
+            dma(((channels + rows) // group + max(group // 2, 1),)),
         ],
         compiler_params=pltpu.CompilerParams(
             collective_id=0, has_side_effects=True, vmem_limit_bytes=40 * 1024 * 1024

time: 73.5 us -> 73.3 us (level)
  no operation moved by 1% of the time
where the time goes in v5:
time: 73.3 us; the launch traced here: 73.2 us
  Pallas kernels  71.5 us (98%)
  local copies, waits for them, and re-layouts  0.97 us (1%)
    pallas_call x1, Pallas kernels, body(): pl.pallas_call(functools.partial(kernel, n, tm_count, sizes), out_shape=p...  71.5 us

profile of v5, /device:TPU:16, one launch (start us, length us, event | category | flops | bytes accessed | tf_op | source)
XLA Modules:
  0.0 73.2 jit_solution(16575340202352111079)
XLA Ops:
  0.7 71.5 %shard_map.55 = bf16[16,256,128]{2,1,0:T(8,128)(2,1)S(1)} custom-call(s32[1,64]{1,0:T(1,128)} %sets_hbm.1, s32[1]{0:T(128)S(6)} %copy.8.delays_hbm, bf16[16,16]{1,0:T(8,128)(2,1)} %taps_hbm.1, bf16[64,192,128]{2,1,0:T(8,128)(2,1)} %bitcast.4, bf16[64,192,128]{2,1,0:T(8,128)(2,1)} %bitcast.5), custom_call_target="tpu_custom_call" | custom-call | tf_op jit(solution)/shard_map/pallas_call | solution.py:413
  72.2 1.0 %copy.7 = bf16[16,2,128,128]{3,2,1,0:T(8,128)(2,1)} copy(bf16[16,2,128,128]{3,2,1,0:T(8,128)(2,1)S(1)} %bitcast.3) | data formatting | bytes 2097152

commit v6 on v5

--- a/solution.py
+++ b/solution.py
@@ -9,7 +9,7 @@
 
 MAXD = 16
 MESH = pl.DeviceIdType.MESH
-LEAD = 16
+GROUPS_AHEAD = 1
 LAG = 16
 
 
@@ -27,6 +27,7 @@
     set_count, tap_count = taps.shape
     head = group if n > 2 else 0
     tail = max(group // 2, 1)
+    lead = GROUPS_AHEAD * group
     bf16, f32 = jnp.bfloat16, jnp.float32
 
     me = lax.axis_index("station")
@@ -114,8 +115,8 @@
         pltpu.make_async_copy(sets_hbm, sets, small_sem.at[2]),
     ]
     first = ahead_channel(0)
-    first_loads = load(first, max(head, group), 0)
-    for copy in first_loads:
+    first_loads, head_loads = load(first, 1, 0), load(first + 1, group - 1, 4)
+    for copy in first_loads + head_loads:
         copy.start()
     for copy in small:
         copy.start()
@@ -205,14 +206,17 @@
         return steered(ch, filtered(filt, window))
 
     def pack(ch):
+        span = pl.ds(ch, group)
         wide = jnp.concatenate(
-            [v_buf[ch, pl.ds(q * fold_rows, fold_rows), :] for q in range(folds)], axis=1
-        )
-        halo_out[ch] = jnp.dot(wide, picker, preferred_element_type=f32).astype(bf16)
-
-        @pl.when(lax.rem(ch, group) == group - 1)
-        def _():
-            halo_copy(ch - (group - 1)).start()
+            [
+                v_buf[span, pl.ds(q * fold_rows, fold_rows), :].reshape(group * fold_rows, time_len)
+                for q in range(folds)
+            ],
+            axis=1,
+        )
+        packed = jnp.dot(wide, picker, preferred_element_type=f32).astype(bf16)
+        halo_out[span] = packed.reshape(group, fold_rows, time_len)
+        halo_copy(ch).start()
 
     def late_rows_of(i):
         ch = ahead_channel(i)
@@ -231,32 +235,36 @@
     present = 2 + jnp.where(me > 0, 1, 0) + jnp.where(me < n - 1, 1, 0)
     pl.semaphore_wait(barrier, present)
 
+    def send_late(i, carry):
+        late_rows_of(i)
+        piece_copy(i, late_rows).start()
+        return carry
+
     if head:
         @pl.when(place == 0)
         def _():
             piece_copy(0, late_rows).start()
 
-            def send_late(i, carry):
-                late_rows_of(i)
-                piece_copy(i, late_rows).start()
-                return carry
+            for copy in head_loads:
+                copy.wait()
 
             lax.fori_loop(1, head, send_late, 0)
 
-            def pack_head(i, carry):
-                pack(ahead_channel(i))
-                return carry
-
-            lax.fori_loop(0, head, pack_head, 0)
+            pack(first)
+
+    @pl.when(place > 0)
+    def _():
+        for copy in head_loads:
+            copy.wait()
 
     for copy in load(0, channels - max(head, group), 2):
         copy.wait()
 
-    def pack_first(i, carry):
-        pack(ahead_channel(i))
+    def pack_first(g, carry):
+        pack(ahead_channel(start + g * group))
         return carry
 
-    lax.fori_loop(start, start + LEAD, pack_first, 0)
+    lax.fori_loop(0, lead // group, pack_first, 0)
 
     if head:
         @pl.when(place == 0)
@@ -283,13 +291,13 @@
     def step(i, carry):
         j = i - offset
 
-        @pl.when(i + LEAD < ahead_count)
-        def _():
-            pack(ahead_channel(i + LEAD))
-
-        @pl.when((j + LEAD >= 0) & (j + LEAD < back_count))
-        def _():
-            pack(back_channel(j + LEAD))
+        @pl.when((i + lead < ahead_count) & (lax.rem(i, group) == 0))
+        def _():
+            pack(ahead_channel(i + lead))
+
+        @pl.when((j + lead >= 0) & (j + lead < back_count) & (lax.rem(j + lead, group) == 0))
+        def _():
+            pack(back_channel(j + lead))
 
         @pl.when(i < ahead_count)
         def _():
@@ -430,7 +438,7 @@
             pltpu.VMEM((channels + rows, time_len, 2 * beams), bf16),
             pltpu.VMEM((rows, time_len, 2 * beams), f32),
             dma((3,)),
-            dma((4,)),
+            dma((6,)),
             dma(()),
             dma((channels // group,)),
             dma(()),

time: 73.3 us -> 73.2 us (level)
  no operation moved by 1% of the time
where the time goes in v6:
time: 73.2 us; the launch traced here: 73 us
  Pallas kernels  71.4 us (98%)
  local copies, waits for them, and re-layouts  0.97 us (1%)
    pallas_call x1, Pallas kernels, body(): pl.pallas_call(functools.partial(kernel, n, tm_count, sizes), out_shape=p...  71.4 us

profile of v6, /device:TPU:16, one launch (start us, length us, event | category | flops | bytes accessed | tf_op | source)
XLA Modules:
  0.0 73.0 jit_solution(826468731169611890)
XLA Ops:
  0.7 71.4 %shard_map.55 = bf16[16,256,128]{2,1,0:T(8,128)(2,1)S(1)} custom-call(s32[1,64]{1,0:T(1,128)} %sets_hbm.1, s32[1]{0:T(128)S(6)} %copy.8.delays_hbm, bf16[16,16]{1,0:T(8,128)(2,1)} %taps_hbm.1, bf16[64,192,128]{2,1,0:T(8,128)(2,1)} %bitcast.4, bf16[64,192,128]{2,1,0:T(8,128)(2,1)} %bitcast.5), custom_call_target="tpu_custom_call" | custom-call | tf_op jit(solution)/shard_map/pallas_call | solution.py:421
  72.1 1.0 %copy.7 = bf16[16,2,128,128]{3,2,1,0:T(8,128)(2,1)} copy(bf16[16,2,128,128]{3,2,1,0:T(8,128)(2,1)S(1)} %bitcast.3) | data formatting | bytes 2097152

commit v7 on v6

--- a/solution.py
+++ b/solution.py
@@ -98,11 +98,12 @@
 
     late_rows, early_rows = pl.ds(pad, time_len - pad), pl.ds(0, pad)
 
-    def piece_copy(i, piece):
+    def piece_copy(i, piece, count=1):
         ch = ahead_channel(i)
+        span = pl.ds(ch, count)
         return pltpu.make_async_remote_copy(
-            src_ref=acc_out.at[ch, piece],
-            dst_ref=acc_in.at[ch, piece],
+            src_ref=acc_out.at[span, piece],
+            dst_ref=acc_in.at[span, piece],
             send_sem=as_sem,
             recv_sem=ar_sem.at[ch // group],
             device_id={"station": me + 1 - 2 * ahead_dir},
@@ -240,6 +241,8 @@
         piece_copy(i, late_rows).start()
         return carry
 
+    cut = jnp.where(lax.axis_index("chan") > 0, min(3, head), head)
+
     if head:
         @pl.when(place == 0)
         def _():
@@ -248,7 +251,7 @@
             for copy in head_loads:
                 copy.wait()
 
-            lax.fori_loop(1, head, send_late, 0)
+            lax.fori_loop(1, cut, send_late, 0)
 
             pack(first)
 
@@ -266,16 +269,12 @@
 
     lax.fori_loop(0, lead // group, pack_first, 0)
 
+
     if head:
         @pl.when(place == 0)
         def _():
             def send_early(i, carry):
                 ch = ahead_channel(i)
-
-                @pl.when(lax.rem(i, group) == 0)
-                def _():
-                    halo_copy(ch).wait_recv()
-
                 m = sets[0, ch]
                 filt = jnp.concatenate(
                     [toeplitz(m, own_lag[early_rows, :]), toeplitz(m, rim_lag[...])], axis=1
@@ -283,10 +282,12 @@
                 window = jnp.concatenate([v_buf[ch], rims_of(ch)], axis=1)
                 total = steered(ch, filtered(filt, window))
                 acc_out[ch, early_rows, :] = total.astype(bf16)
-                piece_copy(i, early_rows).start()
                 return carry
 
+            halo_copy(first).wait_recv()
+            lax.fori_loop(cut, head, send_late, 0)
             lax.fori_loop(0, head, send_early, 0)
+            piece_copy(0, early_rows, head).start()
 
     def step(i, carry):
         j = i - offset

time: 73.2 us -> 73.2 us (level)
  no operation moved by 1% of the time
where the time goes in v7:
time: 73.2 us; the launch traced here: 73 us
  Pallas kernels  71.4 us (98%)
  local copies, waits for them, and re-layouts  0.97 us (1%)
    pallas_call x1, Pallas kernels, body(): pl.pallas_call(functools.partial(kernel, n, tm_count, sizes), out_shape=p...  71.4 us

profile of v7, /device:TPU:16, one launch (start us, length us, event | category | flops | bytes accessed | tf_op | source)
XLA Modules:
  0.0 73.0 jit_solution(10837940165236965843)
XLA Ops:
  0.7 71.4 %shard_map.55 = bf16[16,256,128]{2,1,0:T(8,128)(2,1)S(1)} custom-call(s32[1,64]{1,0:T(1,128)} %sets_hbm.1, s32[1]{0:T(128)S(6)} %copy.8.delays_hbm, bf16[16,16]{1,0:T(8,128)(2,1)} %taps_hbm.1, bf16[64,192,128]{2,1,0:T(8,128)(2,1)} %bitcast.4, bf16[64,192,128]{2,1,0:T(8,128)(2,1)} %bitcast.5), custom_call_target="tpu_custom_call" | custom-call | tf_op jit(solution)/shard_map/pallas_call | solution.py:422
  72.1 1.0 %copy.7 = bf16[16,2,128,128]{3,2,1,0:T(8,128)(2,1)} copy(bf16[16,2,128,128]{3,2,1,0:T(8,128)(2,1)S(1)} %bitcast.3) | data formatting | bytes 2097152

commit v8 on v6

--- a/solution.py
+++ b/solution.py
@@ -131,8 +131,9 @@
     def _():
         pl.semaphore_signal(barrier, inc=1, device_id={"station": me + 1}, device_id_type=MESH)
 
-    for target in ({"tm": earlier}, {"tm": later}):
-        pl.semaphore_signal(barrier, inc=1, device_id=target, device_id_type=MESH)
+    sides = (earlier, later) if tm_count > 2 else (later,)
+    for side in sides:
+        pl.semaphore_signal(barrier, inc=1, device_id={"tm": side}, device_id_type=MESH)
 
     for copy in load(first + max(head, group), rows - max(head, group), 2):
         copy.start()
@@ -232,7 +233,7 @@
         def _():
             late_rows_of(0)
 
-    present = 2 + jnp.where(me > 0, 1, 0) + jnp.where(me < n - 1, 1, 0)
+    present = len(sides) + jnp.where(me > 0, 1, 0) + jnp.where(me < n - 1, 1, 0)
     pl.semaphore_wait(barrier, present)
 
     def send_late(i, carry):

time: 73.2 us -> 73.2 us (level)
  no operation moved by 1% of the time
where the time goes in v8:
time: 73.2 us; the launch traced here: 73 us
  Pallas kernels  71.4 us (98%)
  local copies, waits for them, and re-layouts  0.97 us (1%)
    pallas_call x1, Pallas kernels, body(): pl.pallas_call(functools.partial(kernel, n, tm_count, sizes), out_shape=p...  71.4 us

profile of v8, /device:TPU:16, one launch (start us, length us, event | category | flops | bytes accessed | tf_op | source)
XLA Modules:
  0.0 73.0 jit_solution(16336686865846397161)
XLA Ops:
  0.7 71.4 %shard_map.55 = bf16[16,256,128]{2,1,0:T(8,128)(2,1)S(1)} custom-call(s32[1,64]{1,0:T(1,128)} %sets_hbm.1, s32[1]{0:T(128)S(6)} %copy.8.delays_hbm, bf16[16,16]{1,0:T(8,128)(2,1)} %taps_hbm.1, bf16[64,192,128]{2,1,0:T(8,128)(2,1)} %bitcast.4, bf16[64,192,128]{2,1,0:T(8,128)(2,1)} %bitcast.5), custom_call_target="tpu_custom_call" | custom-call | tf_op jit(solution)/shard_map/pallas_call | solution.py:422
  72.1 1.0 %copy.7 = bf16[16,2,128,128]{3,2,1,0:T(8,128)(2,1)} copy(bf16[16,2,128,128]{3,2,1,0:T(8,128)(2,1)S(1)} %bitcast.3) | data formatting | bytes 2097152

commit v9 on v8

--- a/solution.py
+++ b/solution.py
@@ -395,6 +395,14 @@
 
         lax.fori_loop(0, rows, finish, 0)
         drain()
+
+
+def put_out(pieces, in_ref, out_ref, sem):
+    size = in_ref.shape[0] // pieces
+    for p in range(pieces):
+        span = pl.ds(p * size, size)
+        pltpu.make_async_copy(in_ref.at[span], out_ref.at[span], sem).start()
+    pltpu.make_async_copy(in_ref, out_ref, sem).wait()
 
 
 def body(voltages, delays, tap_sets, tap_table, weights):
@@ -449,6 +457,13 @@
             collective_id=0, has_side_effects=True, vmem_limit_bytes=40 * 1024 * 1024
         ),
     )(*(x if x.ndim == 1 else pltpu.with_memory_space_constraint(x, pltpu.HBM) for x in operands))
+    result = pl.pallas_call(
+        functools.partial(put_out, min(4, rows)),
+        out_shape=pltpu.HBM((rows, 2 * beams, time_len), bf16),
+        in_specs=[pl.BlockSpec(memory_space=pltpu.VMEM)],
+        out_specs=in_hbm,
+        scratch_shapes=[dma(())],
+    )(pltpu.with_memory_space_constraint(result, pltpu.VMEM))
     return result.reshape(rows, 2, beams, time_len)
 
 

time: 73.2 us -> 73.2 us (level)
  Pallas kernels: 71.4 us -> 72.4 us
  local copies, waits for them, and re-layouts: 0.97 us -> 0 us
    unnamed x1 -> x0, local copies, waits for them, and re-layouts: 0.97 us -> none
    pallas_call x0 -> x1, Pallas kernels: none -> 0.97 us  [body(): pl.pallas_call(functools.partial(put_out, min(4, rows)), out_shape=pltpu....]
where the time goes in v9:
time: 73.2 us; the launch traced here: 73 us
  Pallas kernels  72.4 us (99%)
    pallas_call x1, Pallas kernels, body(): pl.pallas_call(functools.partial(kernel, n, tm_count, sizes), out_shape=p...  71.4 us

profile of v9, /device:TPU:16, one launch (start us, length us, event | category | flops | bytes accessed | tf_op | source)
XLA Modules:
  0.0 73.0 jit_solution(12573040743742384637)
XLA Ops:
  0.7 71.4 %shard_map.55.in_ref = bf16[16,256,128]{2,1,0:T(8,128)(2,1)S(1)} custom-call(s32[1,64]{1,0:T(1,128)} %sets_hbm.1, s32[1]{0:T(128)S(6)} %copy.6.delays_hbm, bf16[16,16]{1,0:T(8,128)(2,1)} %taps_hbm.1, bf16[64,192,128]{2,1,0:T(8,128)(2,1)} %bitcast.3, bf16[64,192,128]{2,1,0:T(8,128)(2,1)} %bitcast.4), custom_call_target="tpu_custom_call" | custom-call | tf_op jit(solution)/shard_map/pallas_call | solution.py:430
  72.1 1.0 %shard_map.56 = bf16[16,256,128]{2,1,0:T(8,128)(2,1)} custom-call(bf16[16,256,128]{2,1,0:T(8,128)(2,1)S(1)} %shard_map.55.in_ref), custom_call_target="tpu_custom_call" | custom-call | tf_op jit(solution)/shard_map/pallas_call | solution.py:460
